TPU v7x, 32 devices: a whole 2x2x4 slice. The times are simulated.
32 devices in a mesh: dp: 4 (over x, core), hist: 8 (over z, y).
Axes of the slice: x: 2, y: 2, z: 4, core: 2. Of those that a mesh axis runs over, the one named last changes fastest.
Arguments:
- candidates: bfloat16 [16, 512, 128], P('dp', 'hist'), may hold values from -150 to 150
- history: bfloat16 [16, 16384, 128], P('dp', 'hist'), may hold values from -6 to 6
- projections: bfloat16 [4, 128, 128], P(None, 'dp'), may hold values from -0.5 to 0.5
- lengths: int32 [16], P('dp'), may hold values from 8193 to 16384
- selected: int32 [16, 64], P('dp'), may hold values from 0 to 127, as said below
Outputs:
- interest: bfloat16 [16, 512, 128], P('dp', 'hist')
Inputs may be any that keep to these rules, and one draw needn't show every extreme that they name: `selected`: each row names 64 different history blocks.
All inputs are finite; a program needn't handle non-finite values.
Results may differ from a plain program's by a relative error of at most 0.008.
The roundings to bfloat16 on the way count: a program that leaves them out, or rounds other values in their place, can miss the bound.
Values may be sent and summed in bfloat16 or wider, within the bound.
A program may use at most 128 MiB of HBM per device.

v0:
```python
import math
import jax
import jax.numpy as jnp
from jax import lax
from jax.sharding import PartitionSpec as P

D = 128
H = 4
BLOCK = 128


def scale_heads(blocks, factor):
    layout = blocks.shape
    heads = factor.shape[-1]
    return (blocks.reshape(layout[:-1] + (heads, layout[-1] // heads)) * factor[..., None]).reshape(
        layout
    )


def body(candidates, history, projections, lengths, selected):
    weights = lax.all_gather(projections, "dp", axis=1, tiled=True)
    user_count, own_cands, embed = candidates.shape
    head_size = D // H
    inv_root = 1.0 / math.sqrt(head_size)
    whole = lax.all_gather(candidates, "hist", axis=1, tiled=True)
    queries = jnp.dot(whole.reshape(-1, embed), weights[0], preferred_element_type=jnp.float32)
    queries = queries.astype(jnp.bfloat16).reshape(user_count, -1, embed)
    cand_count = queries.shape[1]
    own_rows = history.shape[1]
    key_value = jnp.concatenate([weights[1], weights[2]], axis=1)
    projected = jnp.dot(history.reshape(-1, embed), key_value, preferred_element_type=jnp.float32)
    projected = projected.astype(jnp.bfloat16).reshape(user_count, own_rows, 2 * embed)
    keys = projected[:, :, :embed]
    values = projected[:, :, embed:]
    places = lax.axis_index("hist") * own_rows + jnp.arange(own_rows, dtype=jnp.int32)
    block_ids = places // BLOCK
    chosen = jnp.any(selected[:, :, None] == block_ids[None, None, :], axis=1)
    live = jnp.logical_and(chosen, places[None, :] < lengths[:, None])
    span = min(512, own_rows)
    pieces = own_rows // span

    def attend(item):
        query_rows, key_rows, value_rows, live_row = item
        query_heads = query_rows.reshape(cand_count, H, head_size)

        def one_piece(sub):
            key_part, value_part, live_part = sub
            scores = (
                jnp.einsum(
                    "chd,khd->hck",
                    query_heads,
                    key_part.reshape(span, H, head_size),
                    preferred_element_type=jnp.float32,
                )
                * inv_root
            )
            scores = jnp.where(live_part[None, None, :], scores, -1e30)
            maxima = jnp.max(scores, axis=-1)
            expo = jnp.where(live_part[None, None, :], jnp.exp(scores - maxima[:, :, None]), 0.0)
            totals = jnp.sum(expo, axis=-1)
            summed = jnp.einsum(
                "hck,khd->chd",
                expo.astype(jnp.bfloat16),
                value_part.reshape(span, H, head_size),
                preferred_element_type=jnp.float32,
            )
            return (maxima.T, totals.T, summed.reshape(cand_count, embed))

        maxima_all, totals_all, summed_all = lax.map(
            one_piece,
            (
                key_rows.reshape(pieces, span, embed),
                value_rows.reshape(pieces, span, embed),
                live_row.reshape(pieces, span),
            ),
        )
        highest = jnp.max(maxima_all, axis=0)
        factors = jnp.exp(maxima_all - highest[None])
        totals = jnp.sum(totals_all * factors, axis=0)
        summed = jnp.sum(scale_heads(summed_all, factors), axis=0)
        return (highest, totals, summed)

    def per_user(item):
        return attend(item)

    maxima, totals, summed = lax.map(per_user, (queries, keys, values, live))
    maxima_all, totals_all, summed_all = (
        lax.all_to_all(maxima[None], "hist", split_axis=2, concat_axis=0, tiled=True),
        lax.all_to_all(totals[None], "hist", split_axis=2, concat_axis=0, tiled=True),
        lax.all_to_all(summed[None], "hist", split_axis=2, concat_axis=0, tiled=True),
    )
    highest = jnp.max(maxima_all, axis=0)
    factors = jnp.exp(maxima_all - highest[None])
    totals = jnp.sum(totals_all * factors, axis=0)
    summed = jnp.sum(scale_heads(summed_all, factors), axis=0)
    attended = scale_heads(summed, 1.0 / totals).astype(jnp.bfloat16)
    interest = jnp.dot(attended.reshape(-1, embed), weights[3], preferred_element_type=jnp.float32)
    return interest.astype(jnp.bfloat16).reshape(user_count, own_cands, embed)


def solution(mesh):
    placed = (
        P("dp", "hist", None),
        P("dp", "hist", None),
        P(None, "dp", None),
        P("dp"),
        P("dp", None),
    )
    return jax.shard_map(
        body, mesh=mesh, in_specs=placed, out_specs=P("dp", "hist", None), check_vma=False
    )
```

profile of v0, /device:TPU:0, one launch (start us, length us, event | category | flops | bytes accessed | tf_op | source)
XLA Modules:
  0.0 321.4 jit_solution(1402405281978077282)
XLA Ops:
  0.0 6.9 %all_gather.6 = bf16[4,128,128]{2,1,0:T(8,128)(2,1)S(1)} all-gather(bf16[4,32,128]{2,1,0:T(8,128)(2,1)} %param.11), channel_id=1, replica_groups=mesh['dp'=4,'hist'=8] {'dp'}, dimensions={1}, use_global_device_ids=true | all-gather | bytes 163840 | tf_op jit(solution)/shard_map/all_gather | solution.py:21
  6.9 3.2 %fusion.12 = bf16[8192,256]{0,1:T(8,128)(2,1)} fusion(bf16[8192,128]{1,0:T(8,128)(2,1)S(1)} %bitcast.121, bf16[128,128]{1,0:T(8,128)(2,1)S(1)} %get-tuple-element.245, bf16[128,128]{1,0:T(8,128)(2,1)S(1)} %get-tuple-element.244), kind=kOutput, calls=%fused_computation.30 | convolution fusion | flops 539099136 | bytes 6356992 | tf_op jit(solution)/shard_map/dot_general | solution.py:31
  10.2 6.4 %copy.83 = bf16[8192,256]{1,0:T(8,128)(2,1)} copy(bf16[8192,256]{0,1:T(8,128)(2,1)} %fusion.12) | data formatting | bytes 8388608 | tf_op jit(solution)/shard_map/reshape | solution.py:32
  16.6 4.5 %fusion.20 = (bf16[4,2048,128]{2,1,0:T(8,128)(2,1)}, bf16[4,2048,128]{2,1,0:T(8,128)(2,1)}) fusion(bf16[4,2048,256]{2,1,0:T(8,128)(2,1)} %bitcast.129), kind=kLoop, calls=%fused_computation.57 | loop fusion | bytes 8388608 | tf_op jit(solution)/shard_map/slice | solution.py:34
  21.1 32.3 %all_gather.7 = bf16[4,512,128]{2,1,0:T(8,128)(2,1)S(1)} all-gather(bf16[4,64,128]{2,1,0:T(8,128)(2,1)S(1)} %copy-done.3), channel_id=1, replica_groups=mesh['dp'=4,'hist'=8] {'hist'}, dimensions={1}, use_global_device_ids=true | all-gather | bytes 589824 | tf_op jit(solution)/shard_map/all_gather | solution.py:25
  55.6 207.6 %while.29 = (s32[]{:T(128)}, f32[4,512,4]{1,2,0:T(4,128)}, f32[4,512,4]{1,2,0:T(4,128)}, f32[4,512,128]{2,0,1:T(4,128)}, bf16[4,2048,128]{2,1,0:T(8,128)(2,1)}, ...) while((s32[]{:T(128)}, f32[4,512,4]{1,2,0:T(4,128)}, ...), condition=%wide.region_9.10_spmd, body=%wide.region_1.9_spmd.sunk | while | flops 148332544 | bytes 36866940 | solution.py:86
  59.5 36.4 %while.30 = (s32[]{:T(128)}, f32[4,512,4]{1,2,0:T(4,128)}, f32[4,512,4]{1,2,0:T(4,128)}, f32[4,512,128]{1,2,0:T(8,128)}, pred[4,512]{1,0:T(4,128)(4,1)S(1)}, /*i...) while((s32[]{:T(128)}, f32[4,512,4]{1,2,0:T(4,128)}, ...), condition=%wide.region_5.5_spmd, body=%wide.region_2.4_spmd.sunk | while | flops 147845120 | bytes 31656596 | solution.py:69
  64.7 3.2 %fusion.40 = f32[4,32,512]{2,1,0:T(8,128)S(1)} fusion(bf16[512,4,32]{0,2,1:T(8,128)(2,1)S(1)} %bitcast.125, f32[4,512,512]{2,1,0:T(8,128)} %copy-done.1, f32[4,512]{1,0:T(4,128)S(1)} %get-tuple-element.380, pred[512]{0:T(512)(128)(4,1)S(1)} %dynamic-slice_reduce_fusion.5), kind=kOutput, calls=%fused_computation.7.clone.1 | convolution fusion | flops 72351744 | bytes 4596224 | tf_op jit(solution)/shard_map/while/body/eval_jaxpr/while/body/eval_jaxpr/hck,khd->chd/dot_general | solution.py:61
  73.7 3.2 %fusion.40 = f32[4,32,512]{2,1,0:T(8,128)S(1)} fusion(bf16[512,4,32]{0,2,1:T(8,128)(2,1)S(1)} %bitcast.125, f32[4,512,512]{2,1,0:T(8,128)} %copy-done.1, f32[4,512]{1,0:T(4,128)S(1)} %get-tuple-element.380, pred[512]{0:T(512)(128)(4,1)S(1)} %dynamic-slice_reduce_fusion.5), kind=kOutput, calls=%fused_computation.7.clone.1 | convolution fusion | flops 72351744 | bytes 4596224 | tf_op jit(solution)/shard_map/while/body/eval_jaxpr/while/body/eval_jaxpr/hck,khd->chd/dot_general | solution.py:61
  82.8 3.2 %fusion.40 = f32[4,32,512]{2,1,0:T(8,128)S(1)} fusion(bf16[512,4,32]{0,2,1:T(8,128)(2,1)S(1)} %bitcast.125, f32[4,512,512]{2,1,0:T(8,128)} %copy-done.1, f32[4,512]{1,0:T(4,128)S(1)} %get-tuple-element.380, pred[512]{0:T(512)(128)(4,1)S(1)} %dynamic-slice_reduce_fusion.5), kind=kOutput, calls=%fused_computation.7.clone.1 | convolution fusion | flops 72351744 | bytes 4596224 | tf_op jit(solution)/shard_map/while/body/eval_jaxpr/while/body/eval_jaxpr/hck,khd->chd/dot_general | solution.py:61
  91.9 3.2 %fusion.40 = f32[4,32,512]{2,1,0:T(8,128)S(1)} fusion(bf16[512,4,32]{0,2,1:T(8,128)(2,1)S(1)} %bitcast.125, f32[4,512,512]{2,1,0:T(8,128)} %copy-done.1, f32[4,512]{1,0:T(4,128)S(1)} %get-tuple-element.380, pred[512]{0:T(512)(128)(4,1)S(1)} %dynamic-slice_reduce_fusion.5), kind=kOutput, calls=%fused_computation.7.clone.1 | convolution fusion | flops 72351744 | bytes 4596224 | tf_op jit(solution)/shard_map/while/body/eval_jaxpr/while/body/eval_jaxpr/hck,khd->chd/dot_general | solution.py:61
  99.6 7.9 %dynamic_update_slice.30 = f32[4,512,128]{2,0,1:T(4,128)} dynamic-update-slice(f32[4,512,128]{2,0,1:T(4,128)} %get-tuple-element.425, f32[1,512,128]{2,0,1:T(1,128)S(1)} %copy.96, s32[]{:T(128)S(6)} %copy.121, s32[]{:T(128)} %constant.66.clone.1..sunk, s32[]{:T(128)} %constant.66.clone.1..sunk) | dynamic-update-slice | bytes 524292 | tf_op jit(solution)/shard_map/while/body/jit(dynamic_update_index_in_dim)/dynamic_update_slice | solution.py:86
  111.4 36.4 %while.30 = (s32[]{:T(128)}, f32[4,512,4]{1,2,0:T(4,128)}, f32[4,512,4]{1,2,0:T(4,128)}, f32[4,512,128]{1,2,0:T(8,128)}, pred[4,512]{1,0:T(4,128)(4,1)S(1)}, /*i...) while((s32[]{:T(128)}, f32[4,512,4]{1,2,0:T(4,128)}, ...), condition=%wide.region_5.5_spmd, body=%wide.region_2.4_spmd.sunk | while | flops 147845120 | bytes 31656596 | solution.py:69
  143.8 3.2 %fusion.40 = f32[4,32,512]{2,1,0:T(8,128)S(1)} fusion(bf16[512,4,32]{0,2,1:T(8,128)(2,1)S(1)} %bitcast.125, f32[4,512,512]{2,1,0:T(8,128)} %copy-done.1, f32[4,512]{1,0:T(4,128)S(1)} %get-tuple-element.380, pred[512]{0:T(512)(128)(4,1)S(1)} %dynamic-slice_reduce_fusion.5), kind=kOutput, calls=%fused_computation.7.clone.1 | convolution fusion | flops 72351744 | bytes 4596224 | tf_op jit(solution)/shard_map/while/body/eval_jaxpr/while/body/eval_jaxpr/hck,khd->chd/dot_general | solution.py:61
  151.5 7.9 %dynamic_update_slice.30 = f32[4,512,128]{2,0,1:T(4,128)} dynamic-update-slice(f32[4,512,128]{2,0,1:T(4,128)} %get-tuple-element.425, f32[1,512,128]{2,0,1:T(1,128)S(1)} %copy.96, s32[]{:T(128)S(6)} %copy.121, s32[]{:T(128)} %constant.66.clone.1..sunk, s32[]{:T(128)} %constant.66.clone.1..sunk) | dynamic-update-slice | bytes 524292 | tf_op jit(solution)/shard_map/while/body/jit(dynamic_update_index_in_dim)/dynamic_update_slice | solution.py:86
  163.3 36.4 %while.30 = (s32[]{:T(128)}, f32[4,512,4]{1,2,0:T(4,128)}, f32[4,512,4]{1,2,0:T(4,128)}, f32[4,512,128]{1,2,0:T(8,128)}, pred[4,512]{1,0:T(4,128)(4,1)S(1)}, /*i...) while((s32[]{:T(128)}, f32[4,512,4]{1,2,0:T(4,128)}, ...), condition=%wide.region_5.5_spmd, body=%wide.region_2.4_spmd.sunk | while | flops 147845120 | bytes 31656596 | solution.py:69
  177.5 3.2 %fusion.40 = f32[4,32,512]{2,1,0:T(8,128)S(1)} fusion(bf16[512,4,32]{0,2,1:T(8,128)(2,1)S(1)} %bitcast.125, f32[4,512,512]{2,1,0:T(8,128)} %copy-done.1, f32[4,512]{1,0:T(4,128)S(1)} %get-tuple-element.380, pred[512]{0:T(512)(128)(4,1)S(1)} %dynamic-slice_reduce_fusion.5), kind=kOutput, calls=%fused_computation.7.clone.1 | convolution fusion | flops 72351744 | bytes 4596224 | tf_op jit(solution)/shard_map/while/body/eval_jaxpr/while/body/eval_jaxpr/hck,khd->chd/dot_general | solution.py:61
  203.4 7.9 %dynamic_update_slice.30 = f32[4,512,128]{2,0,1:T(4,128)} dynamic-update-slice(f32[4,512,128]{2,0,1:T(4,128)} %get-tuple-element.425, f32[1,512,128]{2,0,1:T(1,128)S(1)} %copy.96, s32[]{:T(128)S(6)} %copy.121, s32[]{:T(128)} %constant.66.clone.1..sunk, s32[]{:T(128)} %constant.66.clone.1..sunk) | dynamic-update-slice | bytes 524292 | tf_op jit(solution)/shard_map/while/body/jit(dynamic_update_index_in_dim)/dynamic_update_slice | solution.py:86
  215.2 36.4 %while.30 = (s32[]{:T(128)}, f32[4,512,4]{1,2,0:T(4,128)}, f32[4,512,4]{1,2,0:T(4,128)}, f32[4,512,128]{1,2,0:T(8,128)}, pred[4,512]{1,0:T(4,128)(4,1)S(1)}, /*i...) while((s32[]{:T(128)}, f32[4,512,4]{1,2,0:T(4,128)}, ...), condition=%wide.region_5.5_spmd, body=%wide.region_2.4_spmd.sunk | while | flops 147845120 | bytes 31656596 | solution.py:69
  247.6 3.2 %fusion.40 = f32[4,32,512]{2,1,0:T(8,128)S(1)} fusion(bf16[512,4,32]{0,2,1:T(8,128)(2,1)S(1)} %bitcast.125, f32[4,512,512]{2,1,0:T(8,128)} %copy-done.1, f32[4,512]{1,0:T(4,128)S(1)} %get-tuple-element.380, pred[512]{0:T(512)(128)(4,1)S(1)} %dynamic-slice_reduce_fusion.5), kind=kOutput, calls=%fused_computation.7.clone.1 | convolution fusion | flops 72351744 | bytes 4596224 | tf_op jit(solution)/shard_map/while/body/eval_jaxpr/while/body/eval_jaxpr/hck,khd->chd/dot_general | solution.py:61
  255.3 7.9 %dynamic_update_slice.30 = f32[4,512,128]{2,0,1:T(4,128)} dynamic-update-slice(f32[4,512,128]{2,0,1:T(4,128)} %get-tuple-element.425, f32[1,512,128]{2,0,1:T(1,128)S(1)} %copy.96, s32[]{:T(128)S(6)} %copy.121, s32[]{:T(128)} %constant.66.clone.1..sunk, s32[]{:T(128)} %constant.66.clone.1..sunk) | dynamic-update-slice | bytes 524292 | tf_op jit(solution)/shard_map/while/body/jit(dynamic_update_index_in_dim)/dynamic_update_slice | solution.py:86
  270.5 5.3 %all-to-all-start.2 = ((f32[8,1,1024]{2,1,0:T(1,128)}), f32[8,1,1024]{2,1,0:T(1,128)S(1)}, u32[]{:S(2)}, u32[]{:S(2)}) async-start(f32[8,1,1024]{2,1,0:T(1,128)} %reshape.121), calls=%async_computation.2 | async-start | bytes 65536 | tf_op jit(solution)/shard_map/all_to_all | solution.py:89
  282.5 11.9 %all_to_all.51 = f32[8,1,1024]{2,1,0:T(1,128)S(1)} all-to-all(f32[8,1,1024]{2,1,0:T(1,128)S(1)} %reshape.119), channel_id=1, replica_groups=mesh['dp'=4,'hist'=8] {'hist'}, dimensions={0} | all-to-all | bytes 65536 | tf_op jit(solution)/shard_map/all_to_all | solution.py:88
  294.4 4.4 %all-to-all-start = ((f32[1,4,512,128]{3,1,0,2:T(4,128)}), f32[1,4,512,128]{3,1,0,2:T(4,128)}, u32[]{:S(2)}, u32[]{:S(2)}) async-start(f32[1,4,512,128]{3,1,0,2:T(4,128)} %bitcast.136), calls=%async_computation | async-start | bytes 2097152 | tf_op jit(solution)/shard_map/all_to_all | solution.py:90
  (288 shorter events, 191.4 us)
Async XLA Ops:
  0.0 6.9 %copy-start = (bf16[4,2048,128]{2,1,0:T(8,128)(2,1)S(1)}, bf16[4,2048,128]{2,1,0:T(8,128)(2,1)}, u32[]{:S(2)}) copy-start(bf16[4,2048,128]{2,1,0:T(8,128)(2,1)} %param.10) | copy-start | bytes 6291460
  6.9 46.5 %copy-start.2 = (bf16[4,128,128]{2,1,0:T(8,128)(2,1)}, bf16[4,128,128]{2,1,0:T(8,128)(2,1)S(1)}, u32[]{:S(2)}) copy-start(bf16[4,128,128]{2,1,0:T(8,128)(2,1)S(1)} %all_gather.6) | copy-start | bytes 393220
  16.6 4.5 %copy-start.3 = (bf16[4,64,128]{2,1,0:T(8,128)(2,1)S(1)}, bf16[4,64,128]{2,1,0:T(8,128)(2,1)}, u32[]{:S(2)}) copy-start(bf16[4,64,128]{2,1,0:T(8,128)(2,1)} %param.9) | copy-start | bytes 196612
  16.6 37.9 %copy-start.5 = (s32[4,64]{1,0:T(4,128)S(1)}, s32[4,64]{1,0:T(4,128)}, u32[]{:S(2)}) copy-start(s32[4,64]{1,0:T(4,128)} %param.13) | copy-start | bytes 3076
  16.6 38.3 %copy-start.6 = (s32[4]{0:T(128)S(1)}, s32[4]{0:T(128)}, u32[]{:S(2)}) copy-start(s32[4]{0:T(128)} %param.12) | copy-start | bytes 52
  60.8 1.9 copy-start.1
  69.9 1.9 copy-start.1
  79.0 1.9 copy-start.1
  88.1 1.9 copy-start.1
  112.7 1.9 copy-start.1
  121.8 1.9 copy-start.1
  130.9 1.9 copy-start.1
  140.0 1.9 copy-start.1
  164.6 1.9 copy-start.1
  173.7 1.9 copy-start.1
  182.8 1.9 copy-start.1
  191.9 1.9 copy-start.1
  216.5 1.9 copy-start.1
  225.6 1.9 copy-start.1
  234.7 1.9 copy-start.1
  243.8 1.9 copy-start.1
  263.1 12.7 %copy-start.4 = (f32[4,512,4]{1,2,0:T(4,128)S(1)}, f32[4,512,4]{1,2,0:T(4,128)}, u32[]{:S(2)}) copy-start(f32[4,512,4]{1,2,0:T(4,128)} %get-tuple-element.94) | copy-start | bytes 98308
  270.5 12.0 %all-to-all-start.2 = ((f32[8,1,1024]{2,1,0:T(1,128)}), f32[8,1,1024]{2,1,0:T(1,128)S(1)}, u32[]{:S(2)}, u32[]{:S(2)}) async-start(f32[8,1,1024]{2,1,0:T(1,128)} %reshape.121), calls=%async_computation.2 | async-start | bytes 65536 | tf_op jit(solution)/shard_map/all_to_all | solution.py:89
  294.4 22.8 %all-to-all-start = ((f32[1,4,512,128]{3,1,0,2:T(4,128)}), f32[1,4,512,128]{3,1,0,2:T(4,128)}, u32[]{:S(2)}, u32[]{:S(2)}) async-start(f32[1,4,512,128]{3,1,0,2:T(4,128)} %bitcast.136), calls=%async_computation | async-start | bytes 2097152 | tf_op jit(solution)/shard_map/all_to_all | solution.py:90
where the time goes:
time: 325 us; the launch traced here: 321 us
  local copies, waits for them, and re-layouts  144 us (44%)
  matrix products  75.4 us (23%)
  blocking collectives  51 us (16%)
  other arithmetic  38.9 us (12%)
  starting transfers between devices  9.74 us (3%)
    dynamic_update_slice x44, local copies, waits for them, and re-layouts, body(): maxima, totals, summed = lax.map(per_user, (queries, keys, values, live))  55.9 us
    dot_general x16, matrix products, one_piece(): jnp.einsum('hck,khd->chd', expo.astype(jnp.bfloat16), value_part.reshape(...  51.8 us
    all_gather x1, blocking collectives, body(): whole = lax.all_gather(candidates, 'hist', axis=1, tiled=True)  32.3 us
    while x32, local copies, waits for them, and re-layouts  30.7 us
    dynamic_slice x84, local copies, waits for them, and re-layouts, body(): maxima, totals, summed = lax.map(per_user, (queries, keys, values, live))  19.7 us
    reduce_sum x16, other arithmetic, one_piece(): totals = jnp.sum(expo, axis=-1)  18.6 us
    dot_general x16, matrix products, one_piece(): jnp.einsum('chd,khd->hck', query_heads, key_part.reshape(span, H, head_si...  17.7 us
    unnamed x18, local copies, waits for them, and re-layouts  14.6 us
  transfers between devices with their start and end apart: 2, of which 2 were waited for; matrix products, arithmetic and copies ran while one was open for 7% of the time, Pallas kernels for 0%

commit v1 on v0

--- a/solution.py
+++ b/solution.py
@@ -22,7 +22,12 @@
     user_count, own_cands, embed = candidates.shape
     head_size = D // H
     inv_root = 1.0 / math.sqrt(head_size)
-    whole = lax.all_gather(candidates, "hist", axis=1, tiled=True)
+    ring = [candidates]
+    for hop in range(7):
+        ring.append(lax.ppermute(ring[-1], "hist", [(dev, (dev + 1) % 8) for dev in range(8)]))
+    whole = jnp.roll(
+        jnp.concatenate(ring[::-1], axis=1), (lax.axis_index("hist") + 1) * ring[0].shape[1], axis=1
+    )
     queries = jnp.dot(whole.reshape(-1, embed), weights[0], preferred_element_type=jnp.float32)
     queries = queries.astype(jnp.bfloat16).reshape(user_count, -1, embed)
     cand_count = queries.shape[1]

time: 325 us -> 318 us (0.978)
  blocking collectives: 51 us -> 15.4 us
  waiting for transfers between devices: 1.26 us -> 34 us
  local copies, waits for them, and re-layouts: 144 us -> 138 us
  starting transfers between devices: 9.74 us -> 14.4 us
    all_gather x1 -> x0, blocking collectives: 32.3 us -> none  [body(): whole = lax.all_gather(candidates, 'hist', axis=1, tiled=True)]
    ppermute x0 -> x7, waiting for transfers between devices: none -> 27 us  [body(): lax.ppermute(ring[-1], 'hist', [(dev, (dev + 1) % 8) for dev in range(8)])]
    ppermute x0 -> x7, starting transfers between devices: none -> 6.7 us  [body(): lax.ppermute(ring[-1], 'hist', [(dev, (dev + 1) % 8) for dev in range(8)])]
    all_to_all x1, waiting for transfers between devices: 0.56 us -> 4.16 us  [body(): lax.all_to_all(summed[None], 'hist', split_axis=2, concat_axis=0, tiled=T...]
    unnamed x18 -> x33, local copies, waits for them, and re-layouts: 14.6 us -> 11.3 us
  transfers between devices with their start and end apart: 2 -> 9, of which waited for: 2 -> 7; matrix products, arithmetic and copies ran while one was open for 7% -> 11% of each run, Pallas kernels for 0% -> 0%
where the time goes in v1:
time: 318 us; the launch traced here: 315 us
  local copies, waits for them, and re-layouts  138 us (43%)
  matrix products  75.4 us (24%)
  other arithmetic  36.2 us (11%)
  waiting for transfers between devices  34 us (11%)
  blocking collectives  15.4 us (5%)
  starting transfers between devices  14.4 us (5%)
    dynamic_update_slice x44, local copies, waits for them, and re-layouts, body(): maxima, totals, summed = lax.map(per_user, (queries, keys, values, live))  56 us
    dot_general x16, matrix products, one_piece(): jnp.einsum('hck,khd->chd', expo.astype(jnp.bfloat16), value_part.reshape(...  51.8 us
    while x32, local copies, waits for them, and re-layouts  30.7 us
    ppermute x7, waiting for transfers between devices, body(): lax.ppermute(ring[-1], 'hist', [(dev, (dev + 1) % 8) for dev in range(8)])  27 us
    dynamic_slice x84, local copies, waits for them, and re-layouts, body(): maxima, totals, summed = lax.map(per_user, (queries, keys, values, live))  19.7 us
    reduce_sum x16, other arithmetic, one_piece(): totals = jnp.sum(expo, axis=-1)  18.6 us
    dot_general x16, matrix products, one_piece(): jnp.einsum('chd,khd->hck', query_heads, key_part.reshape(span, H, head_si...  17.8 us
    unnamed x33, local copies, waits for them, and re-layouts  11.3 us
  transfers between devices with their start and end apart: 9, of which 7 were waited for; matrix products, arithmetic and copies ran while one was open for 11% of the time, Pallas kernels for 0%

profile of v1, /device:TPU:0, one launch (start us, length us, event | category | flops | bytes accessed | tf_op | source)
XLA Modules:
  0.0 314.7 jit_solution(10333619185565211002)
XLA Ops:
  3.0 5.6 %all_gather.3 = bf16[4,128,128]{2,1,0:T(8,128)(2,1)S(1)} all-gather(bf16[4,32,128]{2,1,0:T(8,128)(2,1)} %param.11), channel_id=1, replica_groups=mesh['dp'=4,'hist'=8] {'dp'}, dimensions={1}, use_global_device_ids=true | all-gather | bytes 163840 | tf_op jit(solution)/shard_map/all_gather | solution.py:21
  10.2 3.3 %fusion.12 = bf16[8192,256]{0,1:T(8,128)(2,1)} fusion(bf16[8192,128]{1,0:T(8,128)(2,1)S(1)} %bitcast.121, bf16[128,128]{1,0:T(8,128)(2,1)S(1)} %get-tuple-element.245, bf16[128,128]{1,0:T(8,128)(2,1)S(1)} %get-tuple-element.244), kind=kOutput, calls=%fused_computation.30 | convolution fusion | flops 539099136 | bytes 6356992 | tf_op jit(solution)/shard_map/dot_general | solution.py:36
  13.5 6.4 %copy.83 = bf16[8192,256]{1,0:T(8,128)(2,1)} copy(bf16[8192,256]{0,1:T(8,128)(2,1)} %fusion.12) | data formatting | bytes 8388608 | tf_op jit(solution)/shard_map/reshape | solution.py:37
  21.4 4.5 %fusion.20 = (bf16[4,2048,128]{2,1,0:T(8,128)(2,1)}, bf16[4,2048,128]{2,1,0:T(8,128)(2,1)}) fusion(bf16[4,2048,256]{2,1,0:T(8,128)(2,1)} %bitcast.129), kind=kLoop, calls=%fused_computation.74 | loop fusion | bytes 8388608 | tf_op jit(solution)/shard_map/slice | solution.py:39
  27.4 6.3 %collective-permute-done.3 = bf16[4,64,128]{2,1,0:T(8,128)(2,1)S(1)} collective-permute-done((bf16[4,64,128]{2,1,0:T(8,128)(2,1)S(1)}, bf16[4,64,128]{2,1,0:T(8,128)(2,1)S(1)}, u32[]{:S(2)}, u32[]{:S(2)}) %collective-permute-start.3) | collective-permute-done | bytes 65568 | tf_op jit(solution)/shard_map/ppermute | solution.py:27
  34.2 6.6 %collective-permute-done.4 = bf16[4,64,128]{2,1,0:T(8,128)(2,1)S(1)} collective-permute-done((bf16[4,64,128]{2,1,0:T(8,128)(2,1)S(1)}, bf16[4,64,128]{2,1,0:T(8,128)(2,1)S(1)}, u32[]{:S(2)}, u32[]{:S(2)}) %collective-permute-start.4) | collective-permute-done | bytes 65568 | tf_op jit(solution)/shard_map/ppermute | solution.py:27
  40.8 7.0 %collective-permute-done.5 = bf16[4,64,128]{2,1,0:T(8,128)(2,1)S(1)} collective-permute-done((bf16[4,64,128]{2,1,0:T(8,128)(2,1)S(1)}, bf16[4,64,128]{2,1,0:T(8,128)(2,1)S(1)}, u32[]{:S(2)}, u32[]{:S(2)}) %collective-permute-start.5) | collective-permute-done | bytes 65568 | tf_op jit(solution)/shard_map/ppermute | solution.py:27
  48.4 6.3 %collective-permute-done.6 = bf16[4,64,128]{2,1,0:T(8,128)(2,1)S(1)} collective-permute-done((bf16[4,64,128]{2,1,0:T(8,128)(2,1)S(1)}, bf16[4,64,128]{2,1,0:T(8,128)(2,1)S(1)}, u32[]{:S(2)}, u32[]{:S(2)}) %collective-permute-start.6) | collective-permute-done | bytes 65568 | tf_op jit(solution)/shard_map/ppermute | solution.py:27
  56.2 207.7 %while.29 = (s32[]{:T(128)}, f32[4,512,4]{1,2,0:T(4,128)}, f32[4,512,4]{1,2,0:T(4,128)}, f32[4,512,128]{2,0,1:T(4,128)}, bf16[4,2048,128]{2,1,0:T(8,128)(2,1)}, ...) while((s32[]{:T(128)}, f32[4,512,4]{1,2,0:T(4,128)}, ...), condition=%wide.region_9.10_spmd, body=%wide.region_1.9_spmd.sunk | while | flops 148332544 | bytes 36866940 | solution.py:91
  60.1 36.4 %while.30 = (s32[]{:T(128)}, f32[4,512,4]{1,2,0:T(4,128)}, f32[4,512,4]{1,2,0:T(4,128)}, f32[4,512,128]{1,2,0:T(8,128)}, pred[4,512]{1,0:T(4,128)(4,1)S(1)}, /*i...) while((s32[]{:T(128)}, f32[4,512,4]{1,2,0:T(4,128)}, ...), condition=%wide.region_5.5_spmd, body=%wide.region_2.4_spmd.sunk | while | flops 147845120 | bytes 31656596 | solution.py:74
  83.4 3.2 %fusion.40 = f32[4,32,512]{2,1,0:T(8,128)S(1)} fusion(bf16[512,4,32]{0,2,1:T(8,128)(2,1)S(1)} %bitcast.125, f32[4,512,512]{2,1,0:T(8,128)} %copy-done.1, f32[4,512]{1,0:T(4,128)S(1)} %get-tuple-element.380, pred[512]{0:T(512)(128)(4,1)S(1)} %dynamic-slice_reduce_fusion.5), kind=kOutput, calls=%fused_computation.7.clone.1 | convolution fusion | flops 72351744 | bytes 4596224 | tf_op jit(solution)/shard_map/while/body/eval_jaxpr/while/body/eval_jaxpr/hck,khd->chd/dot_general | solution.py:66
  92.5 3.2 %fusion.40 = f32[4,32,512]{2,1,0:T(8,128)S(1)} fusion(bf16[512,4,32]{0,2,1:T(8,128)(2,1)S(1)} %bitcast.125, f32[4,512,512]{2,1,0:T(8,128)} %copy-done.1, f32[4,512]{1,0:T(4,128)S(1)} %get-tuple-element.380, pred[512]{0:T(512)(128)(4,1)S(1)} %dynamic-slice_reduce_fusion.5), kind=kOutput, calls=%fused_computation.7.clone.1 | convolution fusion | flops 72351744 | bytes 4596224 | tf_op jit(solution)/shard_map/while/body/eval_jaxpr/while/body/eval_jaxpr/hck,khd->chd/dot_general | solution.py:66
  100.2 7.9 %dynamic_update_slice.30 = f32[4,512,128]{2,0,1:T(4,128)} dynamic-update-slice(f32[4,512,128]{2,0,1:T(4,128)} %get-tuple-element.425, f32[1,512,128]{2,0,1:T(1,128)S(1)} %copy.96, s32[]{:T(128)S(6)} %copy.136, s32[]{:T(128)} %constant.86.clone.1..sunk, s32[]{:T(128)} %constant.86.clone.1..sunk) | dynamic-update-slice | bytes 524292 | tf_op jit(solution)/shard_map/while/body/jit(dynamic_update_index_in_dim)/dynamic_update_slice | solution.py:91
  112.0 36.4 %while.30 = (s32[]{:T(128)}, f32[4,512,4]{1,2,0:T(4,128)}, f32[4,512,4]{1,2,0:T(4,128)}, f32[4,512,128]{1,2,0:T(8,128)}, pred[4,512]{1,0:T(4,128)(4,1)S(1)}, /*i...) while((s32[]{:T(128)}, f32[4,512,4]{1,2,0:T(4,128)}, ...), condition=%wide.region_5.5_spmd, body=%wide.region_2.4_spmd.sunk | while | flops 147845120 | bytes 31656596 | solution.py:74
  152.1 7.9 %dynamic_update_slice.30 = f32[4,512,128]{2,0,1:T(4,128)} dynamic-update-slice(f32[4,512,128]{2,0,1:T(4,128)} %get-tuple-element.425, f32[1,512,128]{2,0,1:T(1,128)S(1)} %copy.96, s32[]{:T(128)S(6)} %copy.136, s32[]{:T(128)} %constant.86.clone.1..sunk, s32[]{:T(128)} %constant.86.clone.1..sunk) | dynamic-update-slice | bytes 524292 | tf_op jit(solution)/shard_map/while/body/jit(dynamic_update_index_in_dim)/dynamic_update_slice | solution.py:91
  163.9 36.4 %while.30 = (s32[]{:T(128)}, f32[4,512,4]{1,2,0:T(4,128)}, f32[4,512,4]{1,2,0:T(4,128)}, f32[4,512,128]{1,2,0:T(8,128)}, pred[4,512]{1,0:T(4,128)(4,1)S(1)}, /*i...) while((s32[]{:T(128)}, f32[4,512,4]{1,2,0:T(4,128)}, ...), condition=%wide.region_5.5_spmd, body=%wide.region_2.4_spmd.sunk | while | flops 147845120 | bytes 31656596 | solution.py:74
  187.2 3.2 %fusion.40 = f32[4,32,512]{2,1,0:T(8,128)S(1)} fusion(bf16[512,4,32]{0,2,1:T(8,128)(2,1)S(1)} %bitcast.125, f32[4,512,512]{2,1,0:T(8,128)} %copy-done.1, f32[4,512]{1,0:T(4,128)S(1)} %get-tuple-element.380, pred[512]{0:T(512)(128)(4,1)S(1)} %dynamic-slice_reduce_fusion.5), kind=kOutput, calls=%fused_computation.7.clone.1 | convolution fusion | flops 72351744 | bytes 4596224 | tf_op jit(solution)/shard_map/while/body/eval_jaxpr/while/body/eval_jaxpr/hck,khd->chd/dot_general | solution.py:66
  204.0 7.9 %dynamic_update_slice.30 = f32[4,512,128]{2,0,1:T(4,128)} dynamic-update-slice(f32[4,512,128]{2,0,1:T(4,128)} %get-tuple-element.425, f32[1,512,128]{2,0,1:T(1,128)S(1)} %copy.96, s32[]{:T(128)S(6)} %copy.136, s32[]{:T(128)} %constant.86.clone.1..sunk, s32[]{:T(128)} %constant.86.clone.1..sunk) | dynamic-update-slice | bytes 524292 | tf_op jit(solution)/shard_map/while/body/jit(dynamic_update_index_in_dim)/dynamic_update_slice | solution.py:91
  215.9 36.4 %while.30 = (s32[]{:T(128)}, f32[4,512,4]{1,2,0:T(4,128)}, f32[4,512,4]{1,2,0:T(4,128)}, f32[4,512,128]{1,2,0:T(8,128)}, pred[4,512]{1,0:T(4,128)(4,1)S(1)}, /*i...) while((s32[]{:T(128)}, f32[4,512,4]{1,2,0:T(4,128)}, ...), condition=%wide.region_5.5_spmd, body=%wide.region_2.4_spmd.sunk | while | flops 147845120 | bytes 31656596 | solution.py:74
  255.9 7.9 %dynamic_update_slice.30 = f32[4,512,128]{2,0,1:T(4,128)} dynamic-update-slice(f32[4,512,128]{2,0,1:T(4,128)} %get-tuple-element.425, f32[1,512,128]{2,0,1:T(1,128)S(1)} %copy.96, s32[]{:T(128)S(6)} %copy.136, s32[]{:T(128)} %constant.86.clone.1..sunk, s32[]{:T(128)} %constant.86.clone.1..sunk) | dynamic-update-slice | bytes 524292 | tf_op jit(solution)/shard_map/while/body/jit(dynamic_update_index_in_dim)/dynamic_update_slice | solution.py:91
  269.0 3.3 %all-to-all-start.2 = ((f32[8,1,1024]{2,1,0:T(1,128)}), f32[8,1,1024]{2,1,0:T(1,128)S(1)}, u32[]{:S(2)}, u32[]{:S(2)}) async-start(f32[8,1,1024]{2,1,0:T(1,128)} %reshape.121), calls=%async_computation.2 | async-start | bytes 65536 | tf_op jit(solution)/shard_map/all_to_all | solution.py:94
  279.0 9.7 %all_to_all.51 = f32[8,1,1024]{2,1,0:T(1,128)S(1)} all-to-all(f32[8,1,1024]{2,1,0:T(1,128)S(1)} %reshape.119), channel_id=1, replica_groups=mesh['dp'=4,'hist'=8] {'hist'}, dimensions={0} | all-to-all | bytes 65536 | tf_op jit(solution)/shard_map/all_to_all | solution.py:93
  288.7 4.4 %all-to-all-start = ((f32[1,4,512,128]{3,1,0,2:T(4,128)}), f32[1,4,512,128]{3,1,0,2:T(4,128)}, u32[]{:S(2)}, u32[]{:S(2)}) async-start(f32[1,4,512,128]{3,1,0,2:T(4,128)} %bitcast.136), calls=%async_computation | async-start | bytes 2097152 | tf_op jit(solution)/shard_map/all_to_all | solution.py:95
  307.5 4.2 %all-to-all-done = f32[1,4,512,128]{3,1,0,2:T(4,128)} async-done(((f32[1,4,512,128]{3,1,0,2:T(4,128)}), f32[1,4,512,128]{3,1,0,2:T(4,128)}, u32[]{:S(2)}, u32[]{:S(2)}) %all-to-all-start) | async-done | bytes 1048608 | tf_op jit(solution)/shard_map/all_to_all | solution.py:95
  (318 shorter events, 204.8 us)
Async XLA Ops:
  0.0 10.2 %copy-start = (bf16[4,2048,128]{2,1,0:T(8,128)(2,1)S(1)}, bf16[4,2048,128]{2,1,0:T(8,128)(2,1)}, u32[]{:S(2)}) copy-start(bf16[4,2048,128]{2,1,0:T(8,128)(2,1)} %param.10) | copy-start | bytes 6291460
  0.0 8.6 %collective-permute-start = (bf16[4,64,128]{2,1,0:T(8,128)(2,1)}, bf16[4,64,128]{2,1,0:T(8,128)(2,1)S(1)}, u32[]{:S(2)}, u32[]{:S(2)}) collective-permute-start(bf16[4,64,128]{2,1,0:T(8,128)(2,1)} %param.9), channel_id=1, source_target_pairs={{0,1},{1,2},{2,3},{3,4},{4,5},{5,6},{6,7},{7,0},{8,9},{9,10},{10,1... | collective-permute-start | bytes 196616 | tf_op jit(solution)/shard_map/ppermute | solution.py:27
  8.6 46.4 %copy-start.2 = (bf16[4,128,128]{2,1,0:T(8,128)(2,1)}, bf16[4,128,128]{2,1,0:T(8,128)(2,1)S(1)}, u32[]{:S(2)}) copy-start(bf16[4,128,128]{2,1,0:T(8,128)(2,1)S(1)} %all_gather.3) | copy-start | bytes 393220
  8.6 11.2 %collective-permute-start.1 = (bf16[4,64,128]{2,1,0:T(8,128)(2,1)S(1)}, bf16[4,64,128]{2,1,0:T(8,128)(2,1)S(1)}, u32[]{:S(2)}, u32[]{:S(2)}) collective-permute-start(bf16[4,64,128]{2,1,0:T(8,128)(2,1)S(1)} %collective-permute-done), channel_id=1, source_target_pairs={{0,1},{1,2},{2,3},{3,4},{4,5},{5,6},{6,7},{7,0},{8,9},{9,10},{10,1... | collective-permute-start | bytes 196616 | tf_op jit(solution)/shard_map/ppermute | solution.py:27
  19.9 7.0 %collective-permute-start.2 = (bf16[4,64,128]{2,1,0:T(8,128)(2,1)S(1)}, bf16[4,64,128]{2,1,0:T(8,128)(2,1)S(1)}, u32[]{:S(2)}, u32[]{:S(2)}) collective-permute-start(bf16[4,64,128]{2,1,0:T(8,128)(2,1)S(1)} %collective-permute-done.1), channel_id=1, source_target_pairs={{0,1},{1,2},{2,3},{3,4},{4,5},{5,6},{6,7},{7,0},{8,9},{9,10},{10,1... | collective-permute-start | bytes 196616 | tf_op jit(solution)/shard_map/ppermute | solution.py:27
  21.4 12.4 %copy-start.5 = (s32[4,64]{1,0:T(4,128)S(1)}, s32[4,64]{1,0:T(4,128)}, u32[]{:S(2)}) copy-start(s32[4,64]{1,0:T(4,128)} %param.13) | copy-start | bytes 3076
  21.4 26.3 %copy-start.6 = (s32[4]{0:T(128)S(1)}, s32[4]{0:T(128)}, u32[]{:S(2)}) copy-start(s32[4]{0:T(128)} %param.12) | copy-start | bytes 52
  21.4 33.4 %copy-start.3 = (bf16[4,64,128]{2,1,0:T(8,128)(2,1)S(1)}, bf16[4,64,128]{2,1,0:T(8,128)(2,1)}, u32[]{:S(2)}) copy-start(bf16[4,64,128]{2,1,0:T(8,128)(2,1)} %param.9) | copy-start | bytes 196612
  26.8 7.0 %collective-permute-start.3 = (bf16[4,64,128]{2,1,0:T(8,128)(2,1)S(1)}, bf16[4,64,128]{2,1,0:T(8,128)(2,1)S(1)}, u32[]{:S(2)}, u32[]{:S(2)}) collective-permute-start(bf16[4,64,128]{2,1,0:T(8,128)(2,1)S(1)} %collective-permute-done.2), channel_id=1, source_target_pairs={{0,1},{1,2},{2,3},{3,4},{4,5},{5,6},{6,7},{7,0},{8,9},{9,10},{10,1... | collective-permute-start | bytes 196616 | tf_op jit(solution)/shard_map/ppermute | solution.py:27
  33.8 7.0 %collective-permute-start.4 = (bf16[4,64,128]{2,1,0:T(8,128)(2,1)S(1)}, bf16[4,64,128]{2,1,0:T(8,128)(2,1)S(1)}, u32[]{:S(2)}, u32[]{:S(2)}) collective-permute-start(bf16[4,64,128]{2,1,0:T(8,128)(2,1)S(1)} %collective-permute-done.3), channel_id=1, source_target_pairs={{0,1},{1,2},{2,3},{3,4},{4,5},{5,6},{6,7},{7,0},{8,9},{9,10},{10,1... | collective-permute-start | bytes 196616 | tf_op jit(solution)/shard_map/ppermute | solution.py:27
  40.7 7.0 %collective-permute-start.5 = (bf16[4,64,128]{2,1,0:T(8,128)(2,1)S(1)}, bf16[4,64,128]{2,1,0:T(8,128)(2,1)S(1)}, u32[]{:S(2)}, u32[]{:S(2)}) collective-permute-start(bf16[4,64,128]{2,1,0:T(8,128)(2,1)S(1)} %collective-permute-done.4), channel_id=1, source_target_pairs={{0,1},{1,2},{2,3},{3,4},{4,5},{5,6},{6,7},{7,0},{8,9},{9,10},{10,1... | collective-permute-start | bytes 196616 | tf_op jit(solution)/shard_map/ppermute | solution.py:27
  47.7 7.0 %collective-permute-start.6 = (bf16[4,64,128]{2,1,0:T(8,128)(2,1)S(1)}, bf16[4,64,128]{2,1,0:T(8,128)(2,1)S(1)}, u32[]{:S(2)}, u32[]{:S(2)}) collective-permute-start(bf16[4,64,128]{2,1,0:T(8,128)(2,1)S(1)} %collective-permute-done.5), channel_id=1, source_target_pairs={{0,1},{1,2},{2,3},{3,4},{4,5},{5,6},{6,7},{7,0},{8,9},{9,10},{10,1... | collective-permute-start | bytes 196616 | tf_op jit(solution)/shard_map/ppermute | solution.py:27
  61.4 1.9 copy-start.1
  70.5 1.9 copy-start.1
  88.7 1.9 copy-start.1
  113.3 1.9 copy-start.1
  131.5 1.9 copy-start.1
  174.3 1.9 copy-start.1
  192.5 1.9 copy-start.1
  217.2 1.9 copy-start.1
  235.3 1.9 copy-start.1
  263.8 8.5 %copy-start.4 = (f32[4,512,4]{1,2,0:T(4,128)S(1)}, f32[4,512,4]{1,2,0:T(4,128)}, u32[]{:S(2)}) copy-start(f32[4,512,4]{1,2,0:T(4,128)} %get-tuple-element.94) | copy-start | bytes 98308
  269.0 10.0 %all-to-all-start.2 = ((f32[8,1,1024]{2,1,0:T(1,128)}), f32[8,1,1024]{2,1,0:T(1,128)S(1)}, u32[]{:S(2)}, u32[]{:S(2)}) async-start(f32[8,1,1024]{2,1,0:T(1,128)} %reshape.121), calls=%async_computation.2 | async-start | bytes 65536 | tf_op jit(solution)/shard_map/all_to_all | solution.py:94
  288.7 23.0 %all-to-all-start = ((f32[1,4,512,128]{3,1,0,2:T(4,128)}), f32[1,4,512,128]{3,1,0,2:T(4,128)}, u32[]{:S(2)}, u32[]{:S(2)}) async-start(f32[1,4,512,128]{3,1,0,2:T(4,128)} %bitcast.136), calls=%async_computation | async-start | bytes 2097152 | tf_op jit(solution)/shard_map/all_to_all | solution.py:95
  (7 other events, 13.5 us)
